TPU v7x, 256 devices: a whole 4x4x8 slice. The times are simulated.
256 devices in a mesh: section: 16 (over z, core), expert: 16 (over x, y).
Axes of the slice: x: 4, y: 4, z: 8, core: 2. Of those that a mesh axis runs over, the one named last changes fastest.
Arguments:
- state: bfloat16 [16, 2048, 2048], P('section', 'expert'), may hold values from -6 to 6
- norm_gain: float32 [16, 2048], P('section'), may hold values from 0.25 to 1.75
- expert_in: bfloat16 [16, 16, 2048, 1536], P('section', 'expert'), may hold values from -0.125 to 0.125
- expert_out: bfloat16 [16, 16, 768, 2048], P('section', 'expert'), may hold values from -0.21875 to 0.21875
- route_ids: int32 [3, 16, 2048, 6], P(None, 'section', 'expert'), may hold values from 0 to 63, all different within a row
- route_weights: float32 [3, 16, 2048, 6], P(None, 'section', 'expert'), may hold values from 0.3 to 3
Outputs:
- state_out: bfloat16 [16, 2048, 2048], P('section', 'expert')
Inputs may be any that keep to these rules, and one draw needn't show every extreme that they name: `route_ids`: each token names 6 different experts.
All inputs are finite; a program needn't handle non-finite values.
Results may differ from a plain program's by a relative error of at most 0.02.
Values may be sent and summed in bfloat16 or wider, within the bound.
A program may use at most 64 MiB of HBM per device.

v0:
```python
import jax
import jax.numpy as jnp
from jax import lax
from jax.sharding import PartitionSpec as P

epsilon = 1e-06


def shifted(shard, axis, by):
    peers = lax.axis_size(axis)
    return lax.ppermute(shard, axis, [(i, (i + by) % peers) for i in range(peers)])


def normalize(hidden, gain_row):
    widened = hidden.astype(jnp.float32)
    rescale = lax.rsqrt(jnp.mean(widened * widened, axis=-1, keepdims=True) + epsilon)
    return (widened * rescale * gain_row).astype(jnp.bfloat16)


def slot_tables(chosen, experts, capacity):
    window = jnp.arange(experts, dtype=jnp.int32)
    choice_hits = (chosen[:, :, None] == window[None, None, :]).astype(jnp.int32)
    picked = jnp.sum(choice_hits, axis=1)
    rank_table = jnp.cumsum(picked, axis=0) - picked
    kept_table = picked * (rank_table < capacity).astype(jnp.int32)
    slot_index = jnp.arange(capacity, dtype=jnp.int32)
    slot_match = kept_table[:, :, None] * (
        rank_table[:, :, None] == slot_index[None, None, :]
    ).astype(jnp.int32)
    positions = jnp.arange(chosen.shape[0], dtype=jnp.int32)
    token_at = jnp.sum(slot_match * positions[:, None, None], axis=0)
    filled = jnp.sum(slot_match, axis=0)
    kept_hits = choice_hits * kept_table[:, None, :]
    kept_choice = jnp.sum(kept_hits, axis=2)
    flat_slot = jnp.sum(
        kept_hits * (window[None, None, :] * capacity + rank_table[:, None, :]), axis=2
    )
    return (token_at, filled, flat_slot, kept_choice)


def expert_forward(token_rows, inner_weight, outer_weight):
    projected = jnp.dot(token_rows, inner_weight, preferred_element_type=jnp.float32)
    hidden_units = outer_weight.shape[0]
    activated = (jax.nn.silu(projected[:, :hidden_units]) * projected[:, hidden_units:]).astype(
        jnp.bfloat16
    )
    return jnp.dot(activated, outer_weight, preferred_element_type=jnp.float32).astype(jnp.bfloat16)


def on_device(state, norm_gain, expert_in, expert_out, route_ids, route_weights):
    experts = lax.axis_size("expert")
    hidden = state[0]
    capacity = hidden.shape[0] // 4
    gain_row = norm_gain[0]
    inner_weight = expert_in[0, 0]
    outer_weight = expert_out[0, 0]
    for tick_index in range(route_ids.shape[0]):
        chosen = route_ids[tick_index, 0]
        weights = route_weights[tick_index, 0]
        carried = shifted(hidden, "section", 1)
        normed = normalize(hidden, gain_row)
        token_at, filled, flat_slot, kept_choice = slot_tables(chosen, experts, capacity)
        outbound = jnp.take(normed, token_at, axis=0) * filled[:, :, None].astype(jnp.bfloat16)
        arrived_rows = lax.all_to_all(outbound, "expert", split_axis=0, concat_axis=0, tiled=True)
        token_rows = arrived_rows.reshape(-1, arrived_rows.shape[-1])
        served = expert_forward(token_rows, inner_weight, outer_weight)
        returned = lax.all_to_all(
            served.reshape(arrived_rows.shape), "expert", split_axis=0, concat_axis=0, tiled=True
        )
        flat_rows = returned.reshape(-1, returned.shape[-1])
        picked_rows = jnp.take(flat_rows, flat_slot, axis=0)
        mixing = weights * kept_choice.astype(weights.dtype)
        branch = jnp.einsum("tk,tkd->td", mixing, picked_rows.astype(jnp.float32))
        arrived_branch = shifted(branch.astype(jnp.bfloat16), "section", 1).astype(branch.dtype)
        hidden = (carried.astype(jnp.float32) + arrived_branch).astype(jnp.bfloat16)
    return hidden[None]


def solution(mesh):
    in_specs = (
        P("section", "expert", None),
        P("section", None),
        P("section", "expert", None, None),
        P("section", "expert", None, None),
        P(None, "section", "expert", None),
        P(None, "section", "expert", None),
    )
    out_specs = P("section", "expert", None)
    return jax.shard_map(
        on_device, mesh=mesh, in_specs=in_specs, out_specs=out_specs, check_vma=False
    )
```

profile of v0, /device:TPU:96, one launch (start us, length us, event | category | flops | bytes accessed | tf_op | source)
XLA Modules:
  0.0 351.4 jit_solution(9651768424451646065)
XLA Ops:
  0.0 0.9 fusion.70
  0.9 0.6 copy-done.9
  1.6 0.2 reduce_window_sum.20
  1.9 0.6 select_reduce_fusion.2
  2.6 1.2 fusion.36
  3.9 2.0 fusion.38
  5.9 6.3 %gather_fusion = bf16[512,2048]{1,0:T(8,128)(2,1)} fusion(bf16[128,2048]{1,0:T(8,128)(2,1)} %fusion.38, s32[1024]{0:T(1024)S(1)} %pad_clamp_fusion.5), kind=kCustom, calls=%fused_computation.clone | custom fusion | bytes 4196352 | tf_op jit(solution)/shard_map/jit(_take)/gather | solution.py:63
  12.3 3.2 select_multiply_fusion.2
  15.5 7.1 %all-to-all-start = ((bf16[16,32,2048]{2,1,0:T(8,128)(2,1)}), bf16[16,32,2048]{2,1,0:T(8,128)(2,1)}, u32[]{:S(2)}, u32[]{:S(2)}) async-start(bf16[16,32,2048]{2,1,0:T(8,128)(2,1)} %select_multiply_fusion.2), calls=%async_computation | async-start | bytes 4194304 | tf_op jit(solution)/shard_map/all_to_all | solution.py:64
  22.8 0.2 reduce_window_sum.24
  23.1 0.2 reduce_window_sum.25
  23.2 29.8 %all-to-all-done = bf16[16,32,2048]{2,1,0:T(8,128)(2,1)} async-done(((bf16[16,32,2048]{2,1,0:T(8,128)(2,1)}), bf16[16,32,2048]{2,1,0:T(8,128)(2,1)}, u32[]{:S(2)}, u32[]{:S(2)}) %all-to-all-start) | async-done | bytes 2097184 | tf_op jit(solution)/shard_map/all_to_all | solution.py:64
  53.1 6.2 %fusion.4 = f32[512,1536]{1,0:T(8,128)S(1)} fusion(bf16[512,2048]{1,0:T(8,128)(2,1)} %bitcast.5, bf16[1,1,2048,1536]{3,2,1,0:T(8,128)(2,1)} %param.12), kind=kOutput, calls=%fused_computation.10 | convolution fusion | flops 3221225472 | bytes 11534336 | tf_op jit(solution)/shard_map/dot_general | solution.py:42
  59.3 3.2 fusion.21
  62.4 4.6 %all-to-all-start.1 = ((bf16[16,32,2048]{2,1,0:T(8,128)(2,1)}), bf16[16,32,2048]{2,1,0:T(8,128)(2,1)}, u32[]{:S(2)}, u32[]{:S(2)}) async-start(bf16[16,32,2048]{2,1,0:T(8,128)(2,1)} %bitcast.87), calls=%async_computation.1 | async-start | bytes 4194304 | tf_op jit(solution)/shard_map/all_to_all | solution.py:67
  67.0 0.6 compare_select_fusion.1
  67.7 0.9 copy.27
  68.5 0.7 copy.30
  69.3 0.6 broadcast_add_fusion.2
  69.9 0.7 fusion.55
  70.7 0.7 fusion.71
  71.4 0.1 copy.43
  71.8 0.1 copy.19
  72.0 1.3 select_reduce_fusion.1
  73.3 21.3 %all-to-all-done.1 = bf16[16,32,2048]{2,1,0:T(8,128)(2,1)} async-done(((bf16[16,32,2048]{2,1,0:T(8,128)(2,1)}), bf16[16,32,2048]{2,1,0:T(8,128)(2,1)}, u32[]{:S(2)}, u32[]{:S(2)}) %all-to-all-start.1) | async-done | bytes 2097184 | tf_op jit(solution)/shard_map/all_to_all | solution.py:67
  94.6 9.0 %gather_fusion.1 = bf16[768,2048]{1,0:T(8,128)(2,1)} fusion(bf16[512,2048]{1,0:T(8,128)(2,1)} %bitcast.9, s32[1024]{0:T(1024)S(1)} %pad_clamp_fusion.4), kind=kCustom, calls=%fused_computation.1.clone | custom fusion | bytes 6294528 | tf_op jit(solution)/shard_map/jit(_take)/gather | solution.py:71
  103.6 6.3 %reshape.267 = bf16[128,6,2048]{2,1,0:T(8,128)(2,1)} reshape(bf16[768,2048]{1,0:T(8,128)(2,1)} %gather_fusion.1) | data formatting | bytes 6291456 | tf_op jit(solution)/shard_map/jit(_take)/gather | solution.py:71
  109.9 3.5 %fusion.10 = bf16[128,1,2048]{2,1,0:T(2,128)(2,1)S(1)} fusion(bf16[128,6,1]{1,2,0:T(2,128)(2,1)S(1)} %copy.43, bf16[128,6,2048]{2,1,0:T(8,128)(2,1)} %reshape.267, pred[128,6]{1,0:T(8,128)(4,1)S(1)} %copy.19), kind=kOutput, calls=%fused_computation.16 | convolution fusion | flops 4718592 | bytes 3672320 | tf_op jit(solution)/shard_map/tk,tkd->td/dot_general | solution.py:73
  113.4 1.1 copy.78
  114.6 8.8 %collective-permute-done.1 = bf16[128,2048]{1,0:T(8,128)(2,1)} collective-permute-done((bf16[128,2048]{1,0:T(8,128)(2,1)}, bf16[128,2048]{1,0:T(8,128)(2,1)}, u32[]{:S(2)}, u32[]{:S(2)}) %collective-permute-start.1) | collective-permute-done | bytes 524320 | tf_op jit(solution)/shard_map/ppermute | solution.py:11
  123.4 1.5 fusion.39
  124.9 0.8 copy-done.1
  125.7 1.0 fusion.41
  126.6 6.4 %gather_fusion.2 = bf16[512,2048]{1,0:T(8,128)(2,1)} fusion(bf16[128,2048]{1,0:T(8,128)(2,1)} %fusion.41, s32[1024]{0:T(1024)S(1)} %pad_clamp_fusion.3), kind=kCustom, calls=%fused_computation.2.clone | custom fusion | bytes 4196352 | tf_op jit(solution)/shard_map/jit(_take)/gather | solution.py:63
  133.0 1.9 select_multiply_fusion.1
  134.9 33.1 %all_to_all.30 = bf16[16,32,2048]{2,1,0:T(8,128)(2,1)S(1)} all-to-all(bf16[16,32,2048]{2,1,0:T(8,128)(2,1)S(1)} %select_multiply_fusion.1), channel_id=1, replica_groups=mesh['section'=16,'expert'=16] {'expert'}, dimensions={0} | all-to-all | bytes 4194304 | tf_op jit(solution)/shard_map/all_to_all | solution.py:64
  168.0 5.5 %fusion.2 = f32[512,1536]{1,0:T(8,128)S(1)} fusion(bf16[512,2048]{1,0:T(8,128)(2,1)S(1)} %bitcast.90, bf16[1,1,2048,1536]{3,2,1,0:T(8,128)(2,1)} %param.12), kind=kOutput, calls=%fused_computation.8 | convolution fusion | flops 3221225472 | bytes 11534336 | tf_op jit(solution)/shard_map/dot_general | solution.py:42
  173.6 3.1 fusion.24
  176.7 4.8 %all-to-all-start.3 = ((bf16[16,32,2048]{2,1,0:T(8,128)(2,1)}), bf16[16,32,2048]{2,1,0:T(8,128)(2,1)}, u32[]{:S(2)}, u32[]{:S(2)}) async-start(bf16[16,32,2048]{2,1,0:T(8,128)(2,1)} %bitcast.88), calls=%async_computation.3 | async-start | bytes 4194304 | tf_op jit(solution)/shard_map/all_to_all | solution.py:67
  181.8 0.1 copy.45
  182.3 0.6 select_reduce_fusion
  183.0 27.1 %all-to-all-done.3 = bf16[16,32,2048]{2,1,0:T(8,128)(2,1)} async-done(((bf16[16,32,2048]{2,1,0:T(8,128)(2,1)}), bf16[16,32,2048]{2,1,0:T(8,128)(2,1)}, u32[]{:S(2)}, u32[]{:S(2)}) %all-to-all-start.3) | async-done | bytes 2097184 | tf_op jit(solution)/shard_map/all_to_all | solution.py:67
  210.1 9.0 %gather_fusion.3 = bf16[768,2048]{1,0:T(8,128)(2,1)} fusion(bf16[512,2048]{1,0:T(8,128)(2,1)} %bitcast.16, s32[1024]{0:T(1024)S(1)} %pad_clamp_fusion.2), kind=kCustom, calls=%fused_computation.4.clone | custom fusion | bytes 6294528 | tf_op jit(solution)/shard_map/jit(_take)/gather | solution.py:71
  219.1 6.3 %reshape.275 = bf16[128,6,2048]{2,1,0:T(8,128)(2,1)} reshape(bf16[768,2048]{1,0:T(8,128)(2,1)} %gather_fusion.3) | data formatting | bytes 6291456 | tf_op jit(solution)/shard_map/jit(_take)/gather | solution.py:71
  225.4 3.5 %fusion.8 = bf16[128,1,2048]{2,1,0:T(2,128)(2,1)S(1)} fusion(bf16[128,6,1]{1,2,0:T(2,128)(2,1)S(1)} %copy.45, bf16[128,6,2048]{2,1,0:T(8,128)(2,1)} %reshape.275, pred[128,6]{1,0:T(8,128)(4,1)S(1)} %copy.29), kind=kOutput, calls=%fused_computation.14 | convolution fusion | flops 4718592 | bytes 3672320 | tf_op jit(solution)/shard_map/tk,tkd->td/dot_general | solution.py:73
  228.9 1.1 copy.77
  230.1 8.8 %collective-permute-done.3 = bf16[128,2048]{1,0:T(8,128)(2,1)} collective-permute-done((bf16[128,2048]{1,0:T(8,128)(2,1)}, bf16[128,2048]{1,0:T(8,128)(2,1)}, u32[]{:S(2)}, u32[]{:S(2)}) %collective-permute-start.3) | collective-permute-done | bytes 524320 | tf_op jit(solution)/shard_map/ppermute | solution.py:11
  238.9 1.5 fusion.42
  240.4 0.8 copy-done.2
  241.2 1.0 fusion.44
  242.1 6.4 %gather_fusion.4 = bf16[512,2048]{1,0:T(8,128)(2,1)} fusion(bf16[128,2048]{1,0:T(8,128)(2,1)} %fusion.44, s32[1024]{0:T(1024)S(1)} %pad_clamp_fusion.1), kind=kCustom, calls=%fused_computation.3.clone | custom fusion | bytes 4196352 | tf_op jit(solution)/shard_map/jit(_take)/gather | solution.py:63
  248.5 1.9 select_multiply_fusion
  250.4 27.6 %all_to_all.31 = bf16[16,32,2048]{2,1,0:T(8,128)(2,1)S(1)} all-to-all(bf16[16,32,2048]{2,1,0:T(8,128)(2,1)S(1)} %select_multiply_fusion), channel_id=1, replica_groups=mesh['section'=16,'expert'=16] {'expert'}, dimensions={0} | all-to-all | bytes 4194304 | tf_op jit(solution)/shard_map/all_to_all | solution.py:64
  278.0 5.5 %fusion = f32[512,1536]{1,0:T(8,128)S(1)} fusion(bf16[512,2048]{1,0:T(8,128)(2,1)S(1)} %bitcast.91, bf16[1,1,2048,1536]{3,2,1,0:T(8,128)(2,1)} %param.12), kind=kOutput, calls=%fused_computation.6 | convolution fusion | flops 3221225472 | bytes 11534336 | tf_op jit(solution)/shard_map/dot_general | solution.py:42
  283.6 3.1 fusion.27
  286.7 4.8 %all-to-all-start.5 = ((bf16[16,32,2048]{2,1,0:T(8,128)(2,1)}), bf16[16,32,2048]{2,1,0:T(8,128)(2,1)}, u32[]{:S(2)}, u32[]{:S(2)}) async-start(bf16[16,32,2048]{2,1,0:T(8,128)(2,1)} %bitcast.89), calls=%async_computation.5 | async-start | bytes 4194304 | tf_op jit(solution)/shard_map/all_to_all | solution.py:67
  291.7 0.1 copy.47
  292.3 23.4 %all-to-all-done.5 = bf16[16,32,2048]{2,1,0:T(8,128)(2,1)} async-done(((bf16[16,32,2048]{2,1,0:T(8,128)(2,1)}), bf16[16,32,2048]{2,1,0:T(8,128)(2,1)}, u32[]{:S(2)}, u32[]{:S(2)}) %all-to-all-start.5) | async-done | bytes 2097184 | tf_op jit(solution)/shard_map/all_to_all | solution.py:67
  315.6 9.0 %gather_fusion.5 = bf16[768,2048]{1,0:T(8,128)(2,1)} fusion(bf16[512,2048]{1,0:T(8,128)(2,1)} %bitcast.23, s32[1024]{0:T(1024)S(1)} %pad_clamp_fusion), kind=kCustom, calls=%fused_computation.5.clone | custom fusion | bytes 6294528 | tf_op jit(solution)/shard_map/jit(_take)/gather | solution.py:71
  324.6 6.3 %reshape.283 = bf16[128,6,2048]{2,1,0:T(8,128)(2,1)} reshape(bf16[768,2048]{1,0:T(8,128)(2,1)} %gather_fusion.5) | data formatting | bytes 6291456 | tf_op jit(solution)/shard_map/jit(_take)/gather | solution.py:71
  330.9 3.5 %fusion.6 = bf16[128,1,2048]{2,1,0:T(2,128)(2,1)S(1)} fusion(bf16[128,6,1]{1,2,0:T(2,128)(2,1)S(1)} %copy.47, bf16[128,6,2048]{2,1,0:T(8,128)(2,1)} %reshape.283, pred[128,6]{1,0:T(8,128)(4,1)S(1)} %copy.39), kind=kOutput, calls=%fused_computation.12 | convolution fusion | flops 4718592 | bytes 3672320 | tf_op jit(solution)/shard_map/tk,tkd->td/dot_general | solution.py:73
  334.4 0.3 copy.76
  334.8 14.6 %collective-permute-done.5 = bf16[128,2048]{1,0:T(8,128)(2,1)S(1)} collective-permute-done((bf16[128,2048]{1,0:T(8,128)(2,1)S(1)}, bf16[128,2048]{1,0:T(8,128)(2,1)S(1)}, u32[]{:S(2)}, u32[]{:S(2)}) %collective-permute-start.5) | collective-permute-done | bytes 524320 | tf_op jit(solution)/shard_map/ppermute | solution.py:11
  349.4 2.0 fusion.51
  (84 shorter events, 2.4 us)
Async XLA Ops:
  0.0 59.2 %copy-start = (bf16[1,1,768,2048]{3,2,1,0:T(8,128)(2,1)S(1)}, bf16[1,1,768,2048]{3,2,1,0:T(8,128)(2,1)}, u32[]{:S(2)}) copy-start(bf16[1,1,768,2048]{3,2,1,0:T(8,128)(2,1)} %param.13) | copy-start | bytes 9437188
  0.9 0.6 copy-start.9
  15.5 37.6 %all-to-all-start = ((bf16[16,32,2048]{2,1,0:T(8,128)(2,1)}), bf16[16,32,2048]{2,1,0:T(8,128)(2,1)}, u32[]{:S(2)}, u32[]{:S(2)}) async-start(bf16[16,32,2048]{2,1,0:T(8,128)(2,1)} %select_multiply_fusion.2), calls=%async_computation | async-start | bytes 4194304 | tf_op jit(solution)/shard_map/all_to_all | solution.py:64
  22.6 92.0 %collective-permute-start = (bf16[128,2048]{1,0:T(8,128)(2,1)}, bf16[128,2048]{1,0:T(8,128)(2,1)}, u32[]{:S(2)}, u32[]{:S(2)}) collective-permute-start(bf16[128,2048]{1,0:T(8,128)(2,1)} %bitcast.92), channel_id=1, source_target_pairs={{0,16},{16,32},{32,48},{48,64},{64,80},{80,96},{96,112},{112,128},... | collective-permute-start | bytes 1572872 | tf_op jit(solution)/shard_map/ppermute | solution.py:11
  22.6 36.6 %copy-start.5 = (s32[128,6]{0,1:T(8,128)}, s32[128,6]{0,1:T(8,128)S(1)}, u32[]{:S(2)}) copy-start(s32[128,6]{0,1:T(8,128)S(1)} %get-tuple-element.38) | copy-start | bytes 9220
  22.6 36.6 %copy-start.7 = (s32[128,6]{0,1:T(8,128)}, s32[128,6]{0,1:T(8,128)S(1)}, u32[]{:S(2)}) copy-start(s32[128,6]{0,1:T(8,128)S(1)} %get-tuple-element.39) | copy-start | bytes 9220
  62.4 32.2 %all-to-all-start.1 = ((bf16[16,32,2048]{2,1,0:T(8,128)(2,1)}), bf16[16,32,2048]{2,1,0:T(8,128)(2,1)}, u32[]{:S(2)}, u32[]{:S(2)}) async-start(bf16[16,32,2048]{2,1,0:T(8,128)(2,1)} %bitcast.87), calls=%async_computation.1 | async-start | bytes 4194304 | tf_op jit(solution)/shard_map/all_to_all | solution.py:67
  113.4 12.3 %copy-start.4 = (f32[1,2048]{1,0:T(1,128)S(1)}, f32[1,2048]{1,0:T(1,128)}, u32[]{:S(2)}) copy-start(f32[1,2048]{1,0:T(1,128)} %param.11) | copy-start | bytes 24580
  114.5 8.9 %collective-permute-start.1 = (bf16[128,2048]{1,0:T(8,128)(2,1)}, bf16[128,2048]{1,0:T(8,128)(2,1)}, u32[]{:S(2)}, u32[]{:S(2)}) collective-permute-start(bf16[128,2048]{1,0:T(8,128)(2,1)} %bitcast.82), channel_id=1, source_target_pairs={{0,16},{16,32},{32,48},{48,64},{64,80},{80,96},{96,112},{112,128},... | collective-permute-start | bytes 1572872 | tf_op jit(solution)/shard_map/ppermute | solution.py:11
  124.9 0.8 copy-start.1
  176.7 4.9 %copy-start.3 = (s32[128,16]{1,0:T(8,128)S(1)}, s32[128,16]{1,0:T(8,128)}, u32[]{:S(2)}) copy-start(s32[128,16]{1,0:T(8,128)} %get-tuple-element.36) | copy-start | bytes 24580
  176.7 5.0 %copy-start.8 = (s32[128,6]{0,1:T(8,128)S(1)}, s32[128,6]{0,1:T(8,128)}, u32[]{:S(2)}) copy-start(s32[128,6]{0,1:T(8,128)} %copy-done.7) | copy-start | bytes 9220
  176.7 33.4 %all-to-all-start.3 = ((bf16[16,32,2048]{2,1,0:T(8,128)(2,1)}), bf16[16,32,2048]{2,1,0:T(8,128)(2,1)}, u32[]{:S(2)}, u32[]{:S(2)}) async-start(bf16[16,32,2048]{2,1,0:T(8,128)(2,1)} %bitcast.88), calls=%async_computation.3 | async-start | bytes 4194304 | tf_op jit(solution)/shard_map/all_to_all | solution.py:67
  183.0 47.1 %collective-permute-start.2 = (bf16[128,2048]{1,0:T(8,128)(2,1)}, bf16[128,2048]{1,0:T(8,128)(2,1)}, u32[]{:S(2)}, u32[]{:S(2)}) collective-permute-start(bf16[128,2048]{1,0:T(8,128)(2,1)} %copy-done.1), channel_id=1, source_target_pairs={{0,16},{16,32},{32,48},{48,64},{64,80},{80,96},{96,112},{112,128},... | collective-permute-start | bytes 1572872 | tf_op jit(solution)/shard_map/ppermute | solution.py:11
  230.0 8.9 %collective-permute-start.3 = (bf16[128,2048]{1,0:T(8,128)(2,1)}, bf16[128,2048]{1,0:T(8,128)(2,1)}, u32[]{:S(2)}, u32[]{:S(2)}) collective-permute-start(bf16[128,2048]{1,0:T(8,128)(2,1)} %bitcast.81), channel_id=1, source_target_pairs={{0,16},{16,32},{32,48},{48,64},{64,80},{80,96},{96,112},{112,128},... | collective-permute-start | bytes 1572872 | tf_op jit(solution)/shard_map/ppermute | solution.py:11
  240.4 0.8 copy-start.2
  286.7 4.9 %copy-start.6 = (s32[128,6]{0,1:T(8,128)S(1)}, s32[128,6]{0,1:T(8,128)}, u32[]{:S(2)}) copy-start(s32[128,6]{0,1:T(8,128)} %copy-done.5) | copy-start | bytes 9220
  286.7 28.9 %all-to-all-start.5 = ((bf16[16,32,2048]{2,1,0:T(8,128)(2,1)}), bf16[16,32,2048]{2,1,0:T(8,128)(2,1)}, u32[]{:S(2)}, u32[]{:S(2)}) async-start(bf16[16,32,2048]{2,1,0:T(8,128)(2,1)} %bitcast.89), calls=%async_computation.5 | async-start | bytes 4194304 | tf_op jit(solution)/shard_map/all_to_all | solution.py:67
  292.2 42.5 %collective-permute-start.4 = (bf16[128,2048]{1,0:T(8,128)(2,1)}, bf16[128,2048]{1,0:T(8,128)(2,1)}, u32[]{:S(2)}, u32[]{:S(2)}) collective-permute-start(bf16[128,2048]{1,0:T(8,128)(2,1)} %copy-done.2), channel_id=1, source_target_pairs={{0,16},{16,32},{32,48},{48,64},{64,80},{80,96},{96,112},{112,128},... | collective-permute-start | bytes 1572872 | tf_op jit(solution)/shard_map/ppermute | solution.py:11
  334.7 14.7 %collective-permute-start.5 = (bf16[128,2048]{1,0:T(8,128)(2,1)S(1)}, bf16[128,2048]{1,0:T(8,128)(2,1)S(1)}, u32[]{:S(2)}, u32[]{:S(2)}) collective-permute-start(bf16[128,2048]{1,0:T(8,128)(2,1)S(1)} %bitcast.93), channel_id=1, source_target_pairs={{0,16},{16,32},{32,48},{48,64},{64,80},{80,96},{96,112},{112,128},... | collective-permute-start | bytes 1572872 | tf_op jit(solution)/shard_map/ppermute | solution.py:11
where the time goes:
time: 357 us; the launch traced here: 351 us
  waiting for transfers between devices  134 us (38%)
  local copies, waits for them, and re-layouts  75.2 us (21%)
  blocking collectives  60.8 us (17%)
  matrix products  37.2 us (10%)
  other arithmetic  22.4 us (6%)
  starting transfers between devices  21.4 us (6%)
    all_to_all x3, waiting for transfers between devices, on_device(): lax.all_to_all(served.reshape(arrived_rows.shape), 'expert', split_axis=0...  71.8 us
    all_to_all x2, blocking collectives, on_device(): lax.all_to_all(outbound, 'expert', split_axis=0, concat_axis=0, tiled=True)  60.8 us
    gather x6, local copies, waits for them, and re-layouts, on_device(): picked_rows = jnp.take(flat_rows, flat_slot, axis=0)  45.7 us
    ppermute x6, waiting for transfers between devices, shifted(): lax.ppermute(shard, axis, [(i, (i + by) % peers) for i in range(peers)])  32.2 us
    all_to_all x1, waiting for transfers between devices, on_device(): lax.all_to_all(outbound, 'expert', split_axis=0, concat_axis=0, tiled=True)  29.8 us
    gather x3, local copies, waits for them, and re-layouts, on_device(): jnp.take(normed, token_at, axis=0) * filled[:, :, None].astype(jnp.bfloat16)  19.1 us
    dot_general x3, matrix products, expert_forward(): jnp.dot(token_rows, inner_weight, preferred_element_type=jnp.float32)  17.2 us
    all_to_all x3, starting transfers between devices, on_device(): lax.all_to_all(served.reshape(arrived_rows.shape), 'expert', split_axis=0...  14.2 us
  transfers between devices with their start and end apart: 10, of which 7 were waited for; matrix products, arithmetic and copies ran while one was open for 22% of the time, Pallas kernels for 0%

commit v1 on v0

v1 whole, which is shorter than its diff:
```python
import functools

import jax
import jax.numpy as jnp
from jax import lax
from jax.experimental import pallas as pl
from jax.experimental.pallas import tpu as pltpu
from jax.sharding import PartitionSpec as P

MESH = pl.DeviceIdType.MESH
BF16 = jnp.bfloat16
F32 = jnp.float32

EPSILON = 1e-06
SIDE = 4
SLOTS = 32
GROUP = 4
CHUNKS = 4
ORDER = (
    (0, 0), (0, 1), (0, 3), (1, 0), (3, 0), (0, 2), (1, 1), (1, 3),
    (2, 0), (3, 1), (3, 3), (1, 2), (2, 1), (2, 3), (3, 2), (2, 2),
)


def body(
    ids_ref, weights_ref, gain_ref, state_ref, inner_hbm, outer_hbm, out_ref,
    hid, normed, sbuf, rbuf, obuf, ret, acc, ybuf, inner, outer, act, rank_ref, mix_ref, pick, mixing,
    load_sem, weight_sem, out_sem, dispatch_send, dispatch_recv, ret_send, ret_recv, y_send, y_recv,
):
    ticks, tokens = ids_ref.shape[0], ids_ref.shape[2]
    width = gain_ref.shape[1]
    part = width // CHUNKS
    ff = outer.shape[0]
    peers = SIDE * SIDE
    groups = peers // GROUP
    section = lax.axis_index("section")
    sections = lax.axis_size("section")
    me = lax.axis_index("expert")
    my_x, my_y = me // SIDE, lax.rem(me, SIDE)

    def at_offset(dx, dy):
        return lax.rem(my_x + dx + SIDE, SIDE) * SIDE + lax.rem(my_y + dy + SIDE, SIDE)

    target = [at_offset(dx, dy) for dx, dy in ORDER]
    source = [at_offset(-dx, -dy) for dx, dy in ORDER]
    following = lax.rem(section + 1, sections)
    previous = lax.rem(section + sections - 1, sections)

    barrier = pltpu.get_barrier_semaphore()
    for k in range(1, peers):
        pl.semaphore_signal(barrier, 1, device_id={"expert": target[k]}, device_id_type=MESH)
    pl.semaphore_signal(barrier, 1, device_id={"section": following}, device_id_type=MESH)
    pl.semaphore_signal(barrier, 1, device_id={"section": previous}, device_id_type=MESH)

    loads = [
        pltpu.make_async_copy(state_ref.at[:, pl.ds(c * part, part)], hid.at[0, c], load_sem.at[c])
        for c in range(CHUNKS)
    ]
    for load in loads:
        load.start()
    inner_load = pltpu.make_async_copy(inner_hbm, inner, weight_sem.at[0])
    outer_load = pltpu.make_async_copy(outer_hbm, outer, weight_sem.at[1])
    inner_load.start()
    outer_load.start()

    expert_of = lax.broadcasted_iota(jnp.int32, (peers, tokens), 0)
    earlier = (
        lax.broadcasted_iota(jnp.int32, (tokens, tokens), 0)
        < lax.broadcasted_iota(jnp.int32, (tokens, tokens), 1)
    ).astype(F32).astype(BF16)
    slot_of = lax.broadcasted_iota(jnp.int32, (SLOTS, tokens), 0).astype(F32)

    def tables(t, carry):
        ids, weights = ids_ref[t], weights_ref[t]
        picked = jnp.zeros((peers, tokens), F32)
        mix = jnp.zeros((peers, tokens), F32)
        for k in range(ids.shape[0]):
            hit = ids[k : k + 1] == expert_of
            picked = jnp.where(hit, 1.0, picked)
            mix = jnp.where(hit, weights[k : k + 1], mix)
        rank = jnp.dot(picked.astype(BF16), earlier, preferred_element_type=F32)
        rank_ref[...] = jnp.where(picked > 0.0, rank, -1.0)
        mix_ref[...] = mix
        for g in range(groups):
            rows = []
            for j in range(GROUP):
                k = g * GROUP + j
                match = rank_ref[pl.ds(target[k], 1), :] == slot_of
                pick[t, k] = jnp.where(match, 1.0, 0.0).astype(BF16)
                rows.append(jnp.where(match, mix_ref[pl.ds(target[k], 1), :], 0.0))
            mixing[t, g] = jnp.concatenate(rows, axis=0).T.astype(BF16)
        return carry

    lax.fori_loop(0, ticks, tables, 0)
    for load in loads:
        load.wait()
    pl.semaphore_wait(barrier, peers + 1)

    def tick(t, carry):
        squares = jnp.zeros((tokens, 1), F32)
        for c in range(CHUNKS):
            h = hid[t, c].astype(F32)
            squares = squares + jnp.sum(h * h, axis=-1, keepdims=True)
        rescale = lax.rsqrt(squares / width + EPSILON)
        for c in range(CHUNKS):
            columns = slice(c * part, (c + 1) * part)
            normed[:, columns] = (hid[t, c].astype(F32) * rescale * gain_ref[:, columns]).astype(BF16)

        sends = []
        for g in range(groups):
            choose = pick[t, g * GROUP : (g + 1) * GROUP].reshape(GROUP * SLOTS, tokens)
            for c in range(CHUNKS):
                columns = slice(c * part, (c + 1) * part)
                rows = jnp.dot(choose, normed[:, columns], preferred_element_type=F32).astype(BF16)
                for j in range(GROUP):
                    k = g * GROUP + j
                    piece = rows[j * SLOTS : (j + 1) * SLOTS]
                    if k == 0:
                        rbuf[t, 0, :, columns] = piece
                    else:
                        sbuf[k, :, columns] = piece
            for k in range(max(g * GROUP, 1), (g + 1) * GROUP):
                send = pltpu.make_async_remote_copy(
                    sbuf.at[k], rbuf.at[t, k], dispatch_send.at[k], dispatch_recv.at[t, k],
                    device_id={"expert": target[k]}, device_id_type=MESH,
                )
                send.start()
                sends.append(send)

        @pl.when(t == 0)
        def _():
            inner_load.wait()
            outer_load.wait()

        returns = []
        for g in range(groups):
            first = g * GROUP
            for k in range(max(first, 1), first + GROUP):
                sends[k - 1].wait_recv()
            for n in range(ff // 256):
                gate_columns = slice(n * 256, (n + 1) * 256)
                up_columns = slice(ff + n * 256, ff + (n + 1) * 256)
                rows = rbuf[t, first : first + GROUP].reshape(GROUP * SLOTS, width)
                gate = jnp.dot(rows, inner[:, gate_columns], preferred_element_type=F32)
                up = jnp.dot(rows, inner[:, up_columns], preferred_element_type=F32)
                act[:, gate_columns] = (gate / (1.0 + jnp.exp(-gate)) * up).astype(BF16)
            for c in range(CHUNKS):
                served = jnp.dot(
                    act[...], outer[:, c * part : (c + 1) * part], preferred_element_type=F32
                ).astype(BF16)
                for j in range(GROUP):
                    k = first + j
                    piece = served[j * SLOTS : (j + 1) * SLOTS]
                    if k == 0:
                        ret[t, 0, c] = piece
                    else:
                        obuf[k, c] = piece
            for k in range(max(first, 1), first + GROUP):
                send = pltpu.make_async_remote_copy(
                    obuf.at[k], ret.at[t, k], ret_send.at[k], ret_recv.at[t, k],
                    device_id={"expert": source[k]}, device_id_type=MESH,
                )
                send.start()
                returns.append(send)

        moves = []
        for g in range(groups):
            first = g * GROUP
            for k in range(max(first, 1), first + GROUP):
                returns[k - 1].wait_recv()
            for c in range(CHUNKS):
                rows = ret[t, first : first + GROUP, c].reshape(GROUP * SLOTS, part)
                term = jnp.dot(mixing[t, g], rows, preferred_element_type=F32)
                total = (hid[t, c].astype(F32) if g == 0 else acc[c]) + term
                if g < groups - 1:
                    acc[c] = total
                else:
                    ybuf[c] = total.astype(BF16)
                    move = pltpu.make_async_remote_copy(
                        ybuf.at[c], hid.at[t + 1, c], y_send.at[c], y_recv.at[t, c],
                        device_id={"section": following}, device_id_type=MESH,
                    )
                    move.start()
                    moves.append(move)
        for send in sends + returns:
            send.wait_send()
        for move in moves:
            move.wait()
        return carry

    lax.fori_loop(0, ticks, tick, 0)
    stores = [
        pltpu.make_async_copy(hid.at[ticks, c], out_ref.at[:, pl.ds(c * part, part)], out_sem.at[c])
        for c in range(CHUNKS)
    ]
    for store in stores:
        store.start()
    for store in stores:
        store.wait()


def on_device(state, norm_gain, expert_in, expert_out, route_ids, route_weights):
    hidden = state[0]
    tokens, width = hidden.shape
    ticks = route_ids.shape[0]
    ff = expert_out.shape[2]
    peers = SIDE * SIDE
    part = width // CHUNKS
    vmem = pl.BlockSpec(memory_space=pltpu.VMEM)
    hbm = pl.BlockSpec(memory_space=pl.ANY)
    dma = pltpu.SemaphoreType.DMA
    result = pl.pallas_call(
        body,
        out_shape=jax.ShapeDtypeStruct((tokens, width), BF16),
        in_specs=[vmem, vmem, vmem, hbm, hbm, hbm],
        out_specs=hbm,
        scratch_shapes=[
            pltpu.VMEM((ticks + 1, CHUNKS, tokens, part), BF16),
            pltpu.VMEM((tokens, width), BF16),
            pltpu.VMEM((peers, SLOTS, width), BF16),
            pltpu.VMEM((ticks, peers, SLOTS, width), BF16),
            pltpu.VMEM((peers, CHUNKS, SLOTS, part), BF16),
            pltpu.VMEM((ticks, peers, CHUNKS, SLOTS, part), BF16),
            pltpu.VMEM((CHUNKS, tokens, part), F32),
            pltpu.VMEM((CHUNKS, tokens, part), BF16),
            pltpu.VMEM((width, 2 * ff), BF16),
            pltpu.VMEM((ff, width), BF16),
            pltpu.VMEM((GROUP * SLOTS, ff), BF16),
            pltpu.VMEM((peers, tokens), F32),
            pltpu.VMEM((peers, tokens), F32),
            pltpu.VMEM((ticks, peers, SLOTS, tokens), BF16),
            pltpu.VMEM((ticks, peers // GROUP, tokens, GROUP * SLOTS), BF16),
            dma((CHUNKS,)),
            dma((2,)),
            dma((CHUNKS,)),
            dma((peers,)),
            dma((ticks, peers)),
            dma((peers,)),
            dma((ticks, peers)),
            dma((CHUNKS,)),
            dma((ticks, CHUNKS)),
        ],
        compiler_params=pltpu.CompilerParams(
            collective_id=0, has_side_effects=True, vmem_limit_bytes=56 * 1024 * 1024
        ),
    )(
        jnp.swapaxes(route_ids[:, 0], 1, 2),
        jnp.swapaxes(route_weights[:, 0], 1, 2),
        norm_gain,
        hidden,
        expert_in[0, 0],
        expert_out[0, 0],
    )
    return result[None]


def solution(mesh):
    in_specs = (
        P("section", "expert", None),
        P("section", None),
        P("section", "expert", None, None),
        P("section", "expert", None, None),
        P(None, "section", "expert", None),
        P(None, "section", "expert", None),
    )
    out_specs = P("section", "expert", None)
    return jax.shard_map(
        on_device, mesh=mesh, in_specs=in_specs, out_specs=out_specs, check_vma=False
    )
```

time: 357 us -> 203 us (0.57)
  the two profiles are of different devices: /device:TPU:96 before, /device:TPU:138 now
where the time goes in v1:
time: 203 us; the launch traced here: 202 us
  Pallas kernels  198 us (98%)
  local copies, waits for them, and re-layouts  4.48 us (2%)
    pallas_call x1, Pallas kernels, on_device(): pl.pallas_call(body, out_shape=jax.ShapeDtypeStruct((tokens, width), BF16...  198 us
    unnamed x3, local copies, waits for them, and re-layouts  4.48 us

profile of v1, /device:TPU:138, one launch (start us, length us, event | category | flops | bytes accessed | tf_op | source)
XLA Modules:
  0.0 202.5 jit_solution(11794980034405922500)
XLA Ops:
  0.0 1.3 copy.12
  1.3 1.3 copy.11
  2.6 198.0 %shard_map.64 = bf16[128,2048]{1,0:T(8,128)(2,1)} custom-call(s32[3,6,128]{2,1,0:T(8,128)} %bitcast.18, f32[3,6,128]{2,1,0:T(8,128)} %bitcast.19, f32[1,2048]{1,0:T(1,128)} %gain_ref.1, bf16[128,2048]{1,0:T(8,128)(2,1)} %bitcast.17, bf16[2048,1536]{1,0:T(8,128)(2,1)} %bitcast.14, bf16[768,2048]{1,0:T(8,128)(2,1)} %bitcast.15), custom_call_target="tpu_custom_call" | custom-call | tf_op jit(solution)/shard_map/pallas_call | solution.py:212
  200.6 1.9 copy.14

commit v2 on v1

v2 whole, which is shorter than its diff:
```python
import functools

import jax
import jax.numpy as jnp
from jax import lax
from jax.experimental import pallas as pl
from jax.experimental.pallas import tpu as pltpu
from jax.sharding import PartitionSpec as P

MESH = pl.DeviceIdType.MESH
BF16 = jnp.bfloat16
F32 = jnp.float32

EPSILON = 1e-06
SIDE = 4
SLOTS = 32
PIECES = 4
CHUNKS = 4
ORDER = (
    (0, 0), (0, 1), (0, 3), (1, 0), (3, 0), (0, 2), (1, 1), (1, 3),
    (2, 0), (3, 1), (3, 3), (1, 2), (2, 1), (2, 3), (3, 2), (2, 2),
)


def body(
    ids_hbm, weights_hbm, gain_ref, state_ref, inner_hbm, outer_hbm, out_ref,
    ids_own, ids_prev, weights_prev, hid, carried, normed, sbuf, rbuf, obuf, ret, acc,
    inner, outer, act, rank_ref, mix_ref, pick, mixing,
    load_sem, route_sem, weight_sem, out_sem, route_send, route_recv, dispatch_send, dispatch_recv,
    ret_send, ret_recv, carry_send, carry_recv,
):
    ticks, tokens = ids_own.shape[0], ids_own.shape[1]
    width = gain_ref.shape[1]
    part = width // CHUNKS
    ff = outer.shape[0]
    peers = SIDE * SIDE
    piece = SLOTS // PIECES
    batch = peers * piece
    section = lax.axis_index("section")
    sections = lax.axis_size("section")
    me = lax.axis_index("expert")
    my_x, my_y = me // SIDE, lax.rem(me, SIDE)

    def at_offset(dx, dy):
        return lax.rem(my_x + dx + SIDE, SIDE) * SIDE + lax.rem(my_y + dy + SIDE, SIDE)

    target = [at_offset(dx, dy) for dx, dy in ORDER]
    source = [at_offset(-dx, -dy) for dx, dy in ORDER]
    following = lax.rem(section + 1, sections)
    previous = lax.rem(section + sections - 1, sections)

    barrier = pltpu.get_barrier_semaphore()
    for k in range(1, peers):
        pl.semaphore_signal(barrier, 1, device_id={"expert": target[k]}, device_id_type=MESH)
    for k in range(peers):
        for other in (following, previous):
            pl.semaphore_signal(
                barrier, 1, device_id={"section": other, "expert": target[k]}, device_id_type=MESH
            )

    route = pltpu.make_async_copy(ids_hbm, ids_own, route_sem)
    route.start()
    loads = [
        pltpu.make_async_copy(state_ref.at[:, pl.ds(c * part, part)], hid.at[0, c], load_sem.at[c])
        for c in range(CHUNKS)
    ]
    for load in loads:
        load.start()
    inner_load = pltpu.make_async_copy(inner_hbm, inner, weight_sem.at[0])
    outer_load = pltpu.make_async_copy(outer_hbm, outer, weight_sem.at[1])
    inner_load.start()
    outer_load.start()

    expert_of = lax.broadcasted_iota(jnp.int32, (peers, tokens), 0).astype(F32)
    before = lax.broadcasted_iota(jnp.int32, (tokens, tokens), 0)
    after = lax.broadcasted_iota(jnp.int32, (tokens, tokens), 1)
    earlier = jnp.where(before < after, 1.0, 0.0).astype(BF16)
    same = jnp.where(before == after, 1.0, 0.0).astype(BF16)
    slot_of = lax.broadcasted_iota(jnp.int32, (SLOTS, tokens), 0).astype(F32)

    def across(columns):
        return lax.dot_general(
            columns.astype(BF16), same, (((0,), (0,)), ((), ())), preferred_element_type=F32
        )

    def ranks(ids):
        picked = jnp.zeros((peers, tokens), F32)
        for k in range(ids.shape[0]):
            picked = jnp.where(ids[k : k + 1] == expert_of, 1.0, picked)
        rank = jnp.dot(picked.astype(BF16), earlier, preferred_element_type=F32)
        rank_ref[...] = jnp.where(picked > 0.0, rank, -1.0)

    def own_tables(t, carry):
        ranks(across(ids_own[t].astype(F32)))
        for k in range(peers):
            match = rank_ref[pl.ds(target[k], 1), :] == slot_of
            chosen = jnp.where(match, 1.0, 0.0).astype(BF16)
            for g in range(PIECES):
                pick[t, g, k] = chosen[g * piece : (g + 1) * piece]
        return carry

    def previous_tables(t, carry):
        ids, weights = across(ids_prev[t].astype(F32)), across(weights_prev[t])
        ranks(ids)
        mix = jnp.zeros((peers, tokens), F32)
        for k in range(ids.shape[0]):
            mix = jnp.where(ids[k : k + 1] == expert_of, weights[k : k + 1], mix)
        mix_ref[...] = mix
        rows = []
        for k in range(peers):
            match = rank_ref[pl.ds(target[k], 1), :] == slot_of
            rows.append(jnp.where(match, mix_ref[pl.ds(target[k], 1), :], 0.0))
        for g in range(PIECES):
            part_rows = [row[g * piece : (g + 1) * piece] for row in rows]
            mixing[t, g] = jnp.concatenate(part_rows, axis=0).T.astype(BF16)
        return carry

    route.wait()
    lax.fori_loop(0, ticks, own_tables, 0)
    for load in loads:
        load.wait()
    pl.semaphore_wait(barrier, 3 * peers - 1)
    forwards = [
        pltpu.make_async_remote_copy(
            held, landing, route_send.at[i], route_recv.at[i],
            device_id={"section": following}, device_id_type=MESH,
        )
        for i, (held, landing) in enumerate([(ids_hbm, ids_prev), (weights_hbm, weights_prev)])
    ]
    for forward in forwards:
        forward.start()

    def tick(t, carry):
        carry_on = pltpu.make_async_remote_copy(
            hid.at[t], carried.at[t], carry_send, carry_recv.at[t],
            device_id={"section": following}, device_id_type=MESH,
        )
        carry_on.start()
        squares = jnp.zeros((tokens, 1), F32)
        for c in range(CHUNKS):
            h = hid[t, c].astype(F32)
            squares = squares + jnp.sum(h * h, axis=-1, keepdims=True)
        rescale = lax.rsqrt(squares / width + EPSILON)
        for c in range(CHUNKS):
            columns = slice(c * part, (c + 1) * part)
            normed[:, columns] = (hid[t, c].astype(F32) * rescale * gain_ref[:, columns]).astype(BF16)

        sends = {}
        for g in range(PIECES):
            choose = pick[t, g].reshape(batch, tokens)
            for c in range(CHUNKS):
                columns = slice(c * part, (c + 1) * part)
                rows = jnp.dot(choose, normed[:, columns], preferred_element_type=F32).astype(BF16)
                rbuf[t, g, 0, :, columns] = rows[:piece]
                for k in range(1, peers):
                    sbuf[g, k, :, columns] = rows[k * piece : (k + 1) * piece]
            for k in range(1, peers):
                send = pltpu.make_async_remote_copy(
                    sbuf.at[g, k], rbuf.at[t, g, k], dispatch_send.at[g, k], dispatch_recv.at[t, g, k],
                    device_id={"expert": target[k]}, device_id_type=MESH,
                )
                send.start()
                sends[g, k] = send

        @pl.when(t == 0)
        def _():
            inner_load.wait()
            outer_load.wait()

        returns = {}
        for g in range(PIECES):
            for k in range(1, peers):
                sends[g, k].wait_recv()
            for n in range(ff // 256):
                gate_columns = slice(n * 256, (n + 1) * 256)
                up_columns = slice(ff + n * 256, ff + (n + 1) * 256)
                rows = rbuf[t, g].reshape(batch, width)
                gate = jnp.dot(rows, inner[:, gate_columns], preferred_element_type=F32)
                up = jnp.dot(rows, inner[:, up_columns], preferred_element_type=F32)
                act[:, gate_columns] = (gate / (1.0 + jnp.exp(-gate)) * up).astype(BF16)
            for c in range(CHUNKS):
                columns = slice(c * part, (c + 1) * part)
                served = jnp.dot(act[...], outer[:, columns], preferred_element_type=F32).astype(BF16)
                for k in range(peers):
                    obuf[g, k, :, columns] = served[k * piece : (k + 1) * piece]
            for k in range(peers):
                send = pltpu.make_async_remote_copy(
                    obuf.at[g, k], ret.at[t, g, k], ret_send.at[g, k], ret_recv.at[t, g, k],
                    device_id={"section": following, "expert": source[k]}, device_id_type=MESH,
                )
                send.start()
                returns[g, k] = send

        @pl.when(t == 0)
        def _():
            for forward in forwards:
                forward.wait()
            lax.fori_loop(0, ticks, previous_tables, 0)

        carry_on.wait_recv()
        for g in range(PIECES):
            for k in range(peers):
                returns[g, k].wait_recv()
            for c in range(CHUNKS):
                rows = ret[t, g, :, :, c * part : (c + 1) * part].reshape(batch, part)
                term = jnp.dot(mixing[t, g], rows, preferred_element_type=F32)
                total = (carried[t, c].astype(F32) if g == 0 else acc[c]) + term
                if g < PIECES - 1:
                    acc[c] = total
                else:
                    hid[t + 1, c] = total.astype(BF16)
        for send in [*sends.values(), *returns.values(), carry_on]:
            send.wait_send()
        return carry

    lax.fori_loop(0, ticks, tick, 0)
    stores = [
        pltpu.make_async_copy(hid.at[ticks, c], out_ref.at[:, pl.ds(c * part, part)], out_sem.at[c])
        for c in range(CHUNKS)
    ]
    for store in stores:
        store.start()
    for store in stores:
        store.wait()


def on_device(state, norm_gain, expert_in, expert_out, route_ids, route_weights):
    hidden = state[0]
    tokens, width = hidden.shape
    ticks, top = route_ids.shape[0], route_ids.shape[3]
    ff = expert_out.shape[2]
    peers = SIDE * SIDE
    piece = SLOTS // PIECES
    part = width // CHUNKS
    vmem = pl.BlockSpec(memory_space=pltpu.VMEM)
    hbm = pl.BlockSpec(memory_space=pl.ANY)
    dma = pltpu.SemaphoreType.DMA
    result = pl.pallas_call(
        body,
        out_shape=jax.ShapeDtypeStruct((tokens, width), BF16),
        in_specs=[hbm, hbm, vmem, hbm, hbm, hbm],
        out_specs=hbm,
        scratch_shapes=[
            pltpu.VMEM((ticks, tokens, top), jnp.int32),
            pltpu.VMEM((ticks, tokens, top), jnp.int32),
            pltpu.VMEM((ticks, tokens, top), F32),
            pltpu.VMEM((ticks + 1, CHUNKS, tokens, part), BF16),
            pltpu.VMEM((ticks, CHUNKS, tokens, part), BF16),
            pltpu.VMEM((tokens, width), BF16),
            pltpu.VMEM((PIECES, peers, piece, width), BF16),
            pltpu.VMEM((ticks, PIECES, peers, piece, width), BF16),
            pltpu.VMEM((PIECES, peers, piece, width), BF16),
            pltpu.VMEM((ticks, PIECES, peers, piece, width), BF16),
            pltpu.VMEM((CHUNKS, tokens, part), F32),
            pltpu.VMEM((width, 2 * ff), BF16),
            pltpu.VMEM((ff, width), BF16),
            pltpu.VMEM((peers * piece, ff), BF16),
            pltpu.VMEM((peers, tokens), F32),
            pltpu.VMEM((peers, tokens), F32),
            pltpu.VMEM((ticks, PIECES, peers, piece, tokens), BF16),
            pltpu.VMEM((ticks, PIECES, tokens, peers * piece), BF16),
            dma((CHUNKS,)),
            dma(()),
            dma((2,)),
            dma((CHUNKS,)),
            dma((2,)),
            dma((2,)),
            dma((PIECES, peers)),
            dma((ticks, PIECES, peers)),
            dma((PIECES, peers)),
            dma((ticks, PIECES, peers)),
            dma(()),
            dma((ticks,)),
        ],
        compiler_params=pltpu.CompilerParams(
            collective_id=0, has_side_effects=True, vmem_limit_bytes=56 * 1024 * 1024
        ),
    )(
        route_ids[:, 0],
        route_weights[:, 0],
        norm_gain,
        hidden,
        expert_in[0, 0],
        expert_out[0, 0],
    )
    return result[None]


def solution(mesh):
    in_specs = (
        P("section", "expert", None),
        P("section", None),
        P("section", "expert", None, None),
        P("section", "expert", None, None),
        P(None, "section", "expert", None),
        P(None, "section", "expert", None),
    )
    out_specs = P("section", "expert", None)
    return jax.shard_map(
        on_device, mesh=mesh, in_specs=in_specs, out_specs=out_specs, check_vma=False
    )
```

time: 203 us -> 168 us (0.83)
  the two profiles are of different devices: /device:TPU:138 before, /device:TPU:96 now
where the time goes in v2:
time: 168 us; the launch traced here: 167 us
  Pallas kernels  162 us (96%)
  local copies, waits for them, and re-layouts  4.91 us (3%)
    pallas_call x1, Pallas kernels, on_device(): pl.pallas_call(body, out_shape=jax.ShapeDtypeStruct((tokens, width), BF16...  162 us
    unnamed x3, local copies, waits for them, and re-layouts  4.91 us

profile of v2, /device:TPU:96, one launch (start us, length us, event | category | flops | bytes accessed | tf_op | source)
XLA Modules:
  0.0 166.9 jit_solution(10591903298770796124)
XLA Ops:
  0.0 1.5 copy.7
  1.5 1.5 copy.8
  3.0 162.0 %shard_map.64 = bf16[128,2048]{1,0:T(8,128)(2,1)} custom-call(s32[3,128,6]{2,1,0:T(8,128)} %bitcast.9, f32[3,128,6]{2,1,0:T(8,128)} %bitcast.10, f32[1,2048]{1,0:T(1,128)} %gain_ref.1, bf16[128,2048]{1,0:T(8,128)(2,1)} %bitcast.11, bf16[2048,1536]{1,0:T(8,128)(2,1)} %bitcast.6, bf16[768,2048]{1,0:T(8,128)(2,1)} %bitcast.7), custom_call_target="tpu_custom_call" | custom-call | tf_op jit(solution)/shard_map/pallas_call | solution.py:238
  165.0 1.9 %copy.10 = bf16[1,128,2048]{2,1,0:T(8,128)(2,1)} copy(bf16[1,128,2048]{2,1,0:T(8,128)(2,1)} %bitcast.8) | data formatting | bytes 1048576

commit v3 on v2

--- a/solution.py
+++ b/solution.py
@@ -29,7 +29,7 @@
     load_sem, route_sem, weight_sem, out_sem, route_send, route_recv, dispatch_send, dispatch_recv,
     ret_send, ret_recv, carry_send, carry_recv,
 ):
-    ticks, tokens = ids_own.shape[0], ids_own.shape[1]
+    ticks, top, _, tokens = ids_own.shape
     width = gain_ref.shape[1]
     part = width // CHUNKS
     ff = outer.shape[0]
@@ -71,27 +71,21 @@
     inner_load.start()
     outer_load.start()
 
-    expert_of = lax.broadcasted_iota(jnp.int32, (peers, tokens), 0).astype(F32)
+    expert_of = lax.broadcasted_iota(jnp.int32, (peers, tokens), 0)
     before = lax.broadcasted_iota(jnp.int32, (tokens, tokens), 0)
     after = lax.broadcasted_iota(jnp.int32, (tokens, tokens), 1)
     earlier = jnp.where(before < after, 1.0, 0.0).astype(BF16)
-    same = jnp.where(before == after, 1.0, 0.0).astype(BF16)
     slot_of = lax.broadcasted_iota(jnp.int32, (SLOTS, tokens), 0).astype(F32)
-
-    def across(columns):
-        return lax.dot_general(
-            columns.astype(BF16), same, (((0,), (0,)), ((), ())), preferred_element_type=F32
-        )
 
     def ranks(ids):
         picked = jnp.zeros((peers, tokens), F32)
-        for k in range(ids.shape[0]):
-            picked = jnp.where(ids[k : k + 1] == expert_of, 1.0, picked)
+        for k in range(top):
+            picked = jnp.where(ids[k] == expert_of, 1.0, picked)
         rank = jnp.dot(picked.astype(BF16), earlier, preferred_element_type=F32)
         rank_ref[...] = jnp.where(picked > 0.0, rank, -1.0)
 
     def own_tables(t, carry):
-        ranks(across(ids_own[t].astype(F32)))
+        ranks([ids_own[t, k] for k in range(top)])
         for k in range(peers):
             match = rank_ref[pl.ds(target[k], 1), :] == slot_of
             chosen = jnp.where(match, 1.0, 0.0).astype(BF16)
@@ -100,11 +94,11 @@
         return carry
 
     def previous_tables(t, carry):
-        ids, weights = across(ids_prev[t].astype(F32)), across(weights_prev[t])
+        ids = [ids_prev[t, k] for k in range(top)]
         ranks(ids)
         mix = jnp.zeros((peers, tokens), F32)
-        for k in range(ids.shape[0]):
-            mix = jnp.where(ids[k : k + 1] == expert_of, weights[k : k + 1], mix)
+        for k in range(top):
+            mix = jnp.where(ids[k] == expert_of, weights_prev[t, k], mix)
         mix_ref[...] = mix
         rows = []
         for k in range(peers):
@@ -119,7 +113,6 @@
     lax.fori_loop(0, ticks, own_tables, 0)
     for load in loads:
         load.wait()
-    pl.semaphore_wait(barrier, 3 * peers - 1)
     forwards = [
         pltpu.make_async_remote_copy(
             held, landing, route_send.at[i], route_recv.at[i],
@@ -127,15 +120,8 @@
         )
         for i, (held, landing) in enumerate([(ids_hbm, ids_prev), (weights_hbm, weights_prev)])
     ]
-    for forward in forwards:
-        forward.start()
 
     def tick(t, carry):
-        carry_on = pltpu.make_async_remote_copy(
-            hid.at[t], carried.at[t], carry_send, carry_recv.at[t],
-            device_id={"section": following}, device_id_type=MESH,
-        )
-        carry_on.start()
         squares = jnp.zeros((tokens, 1), F32)
         for c in range(CHUNKS):
             h = hid[t, c].astype(F32)
@@ -145,6 +131,10 @@
             columns = slice(c * part, (c + 1) * part)
             normed[:, columns] = (hid[t, c].astype(F32) * rescale * gain_ref[:, columns]).astype(BF16)
 
+        carry_on = pltpu.make_async_remote_copy(
+            hid.at[t], carried.at[t], carry_send, carry_recv.at[t],
+            device_id={"section": following}, device_id_type=MESH,
+        )
         sends = {}
         for g in range(PIECES):
             choose = pick[t, g].reshape(batch, tokens)
@@ -154,13 +144,27 @@
                 rbuf[t, g, 0, :, columns] = rows[:piece]
                 for k in range(1, peers):
                     sbuf[g, k, :, columns] = rows[k * piece : (k + 1) * piece]
-            for k in range(1, peers):
+            if g == 0:
+
+                @pl.when(t == 0)
+                def _():
+                    pl.semaphore_wait(barrier, 3 * peers - 1)
+
+            for k in (reversed(range(1, peers)) if g == PIECES - 1 else range(1, peers)):
                 send = pltpu.make_async_remote_copy(
                     sbuf.at[g, k], rbuf.at[t, g, k], dispatch_send.at[g, k], dispatch_recv.at[t, g, k],
                     device_id={"expert": target[k]}, device_id_type=MESH,
                 )
                 send.start()
                 sends[g, k] = send
+            if g == 0:
+                carry_on.start()
+
+                @pl.when(t == 0)
+                def _():
+                    for forward in forwards:
+                        forward.start()
+
 
         @pl.when(t == 0)
         def _():
@@ -183,7 +187,7 @@
                 served = jnp.dot(act[...], outer[:, columns], preferred_element_type=F32).astype(BF16)
                 for k in range(peers):
                     obuf[g, k, :, columns] = served[k * piece : (k + 1) * piece]
-            for k in range(peers):
+            for k in (reversed(range(peers)) if g == PIECES - 1 else range(peers)):
                 send = pltpu.make_async_remote_copy(
                     obuf.at[g, k], ret.at[t, g, k], ret_send.at[g, k], ret_recv.at[t, g, k],
                     device_id={"section": following, "expert": source[k]}, device_id_type=MESH,
@@ -241,9 +245,9 @@
         in_specs=[hbm, hbm, vmem, hbm, hbm, hbm],
         out_specs=hbm,
         scratch_shapes=[
-            pltpu.VMEM((ticks, tokens, top), jnp.int32),
-            pltpu.VMEM((ticks, tokens, top), jnp.int32),
-            pltpu.VMEM((ticks, tokens, top), F32),
+            pltpu.VMEM((ticks, top, 1, tokens), jnp.int32),
+            pltpu.VMEM((ticks, top, 1, tokens), jnp.int32),
+            pltpu.VMEM((ticks, top, 1, tokens), F32),
             pltpu.VMEM((ticks + 1, CHUNKS, tokens, part), BF16),
             pltpu.VMEM((ticks, CHUNKS, tokens, part), BF16),
             pltpu.VMEM((tokens, width), BF16),
@@ -276,8 +280,8 @@
             collective_id=0, has_side_effects=True, vmem_limit_bytes=56 * 1024 * 1024
         ),
     )(
-        route_ids[:, 0],
-        route_weights[:, 0],
+        jnp.transpose(route_ids, (0, 3, 1, 2)),
+        jnp.transpose(route_weights, (0, 3, 1, 2)),
         norm_gain,
         hidden,
         expert_in[0, 0],

time: 168 us -> 160 us (0.952)
  the two profiles are of different devices: /device:TPU:96 before, /device:TPU:66 now
where the time goes in v3:
time: 160 us
  Pallas kernels  158 us (99%)
  local copies, waits for them, and re-layouts  1.88 us (1%)
    pallas_call x1, Pallas kernels, on_device(): pl.pallas_call(body, out_shape=jax.ShapeDtypeStruct((tokens, width), BF16...  158 us

profile of v3, /device:TPU:66, one launch (start us, length us, event | category | flops | bytes accessed | tf_op | source)
XLA Modules:
  0.0 159.8 jit_solution(16400329472875130378)
XLA Ops:
  0.0 157.9 %shard_map.64 = bf16[128,2048]{1,0:T(8,128)(2,1)} custom-call(s32[3,6,1,128]{3,2,1,0:T(1,128)} %bitcast.10, f32[3,6,1,128]{3,2,1,0:T(1,128)} %bitcast.11, f32[1,2048]{1,0:T(1,128)} %gain_ref.1, bf16[128,2048]{1,0:T(8,128)(2,1)} %bitcast.9, bf16[2048,1536]{1,0:T(8,128)(2,1)} %bitcast.6, bf16[768,2048]{1,0:T(8,128)(2,1)} %bitcast.7), custom_call_target="tpu_custom_call" | custom-call | tf_op jit(solution)/shard_map/pallas_call | solution.py:242
  157.9 1.9 %copy.8 = bf16[1,128,2048]{2,1,0:T(8,128)(2,1)} copy(bf16[1,128,2048]{2,1,0:T(8,128)(2,1)} %bitcast.8) | data formatting | bytes 1048576

commit v4 on v3

v4 whole, which is shorter than its diff:
```python
import functools

import jax
import jax.numpy as jnp
from jax import lax
from jax.experimental import pallas as pl
from jax.experimental.pallas import tpu as pltpu
from jax.sharding import PartitionSpec as P

MESH = pl.DeviceIdType.MESH
BF16 = jnp.bfloat16
F32 = jnp.float32

EPSILON = 1e-06
SIDE = 4
SLOTS = 32
HALVES = 2
CHUNKS = 4
RETURNS = 4
ORDER = (
    (0, 0), (0, 1), (0, 3), (1, 0), (3, 0), (0, 2), (1, 1), (1, 3),
    (2, 0), (3, 1), (3, 3), (1, 2), (2, 1), (2, 3), (3, 2), (2, 2),
)
NEAR = ((0, 0), (0, 1), (0, 3), (1, 0), (0, 2), (1, 1), (1, 3), (1, 2))


def body(
    ids_hbm, weights_hbm, gain_ref, state_ref, inner_hbm, outer_hbm, out_ref,
    ids_own, ids_prev, weights_prev, ids_pair, hid, carried, normed, dense, sbuf, rbuf, obuf, ret, acc,
    inner, outer, act, rank_ref, mix_ref, pick, mixing,
    load_sem, route_sem, weight_sem, out_sem, route_send, route_recv, pair_send, pair_recv,
    dense_send, dense_recv, dispatch_send, dispatch_recv, ret_send, ret_recv, carry_send, carry_recv,
):
    ticks, top, _, tokens = ids_own.shape
    width = gain_ref.shape[1]
    part = width // CHUNKS
    ret_part = width // RETURNS
    ff = outer.shape[0]
    peers = SIDE * SIDE
    half = SLOTS // HALVES
    batch = peers * half
    section = lax.axis_index("section")
    sections = lax.axis_size("section")
    me = lax.axis_index("expert")
    my_x, my_y = me // SIDE, lax.rem(me, SIDE)

    def wrap(value):
        return lax.rem(value + 2 * SIDE, SIDE)

    def at_offset(dx, dy):
        return wrap(my_x + dx) * SIDE + wrap(my_y + dy)

    target = [at_offset(k // SIDE, k % SIDE) for k in range(peers)]
    source = [at_offset(-(k // SIDE), -(k % SIDE)) for k in range(peers)]
    order = [dx * SIDE + dy for dx, dy in ORDER]
    following = lax.rem(section + 1, sections)
    previous = lax.rem(section + sections - 1, sections)

    step_x, step_y = 1 - 2 * lax.rem(my_x, 2), 1 - 2 * lax.rem(my_y, 2)
    steps = [step_x, -step_x, step_y, -step_y]
    partner, near_target, near_index = [], [], []
    for c, step in enumerate(steps):
        along = c < CHUNKS // 2

        def offset(lengthwise, across, along=along):
            return (lengthwise, across) if along else (across, lengthwise)

        partner.append(at_offset(*offset(step, 0)))
        near_target.append([at_offset(*offset(-step * away, across)) for away, across in NEAR])
        indices = []
        for owner in range(2):
            pairs = [offset(wrap(-step * (away + owner)), across) for away, across in NEAR]
            indices.append([dx * SIDE + dy for dx, dy in pairs])
        near_index.append(indices)

    barrier = pltpu.get_barrier_semaphore()
    for k in range(1, peers):
        pl.semaphore_signal(barrier, 1, device_id={"expert": target[k]}, device_id_type=MESH)
    for k in range(peers):
        for other in (following, previous):
            pl.semaphore_signal(
                barrier, 1, device_id={"section": other, "expert": target[k]}, device_id_type=MESH
            )

    route = pltpu.make_async_copy(ids_hbm, ids_own, route_sem)
    route.start()
    loads = [
        pltpu.make_async_copy(state_ref.at[:, pl.ds(c * part, part)], hid.at[0, c], load_sem.at[c])
        for c in range(CHUNKS)
    ]
    for load in loads:
        load.start()
    inner_load = pltpu.make_async_copy(inner_hbm, inner, weight_sem.at[0])
    outer_load = pltpu.make_async_copy(outer_hbm, outer, weight_sem.at[1])
    inner_load.start()
    outer_load.start()

    expert_of = lax.broadcasted_iota(jnp.int32, (peers, tokens), 0)
    before = lax.broadcasted_iota(jnp.int32, (tokens, tokens), 0)
    after = lax.broadcasted_iota(jnp.int32, (tokens, tokens), 1)
    earlier = jnp.where(before < after, 1.0, 0.0).astype(BF16)
    slot_of = lax.broadcasted_iota(jnp.int32, (SLOTS, tokens), 0).astype(F32)

    def ranks(ids):
        picked = jnp.zeros((peers, tokens), F32)
        for k in range(top):
            picked = jnp.where(ids[k] == expert_of, 1.0, picked)
        rank = jnp.dot(picked.astype(BF16), earlier, preferred_element_type=F32)
        rank_ref[...] = jnp.where(picked > 0.0, rank, -1.0)

    def choose(t, owner, c):
        for j in range(len(NEAR)):
            match = rank_ref[pl.ds(near_target[c][j], 1), :] == slot_of
            chosen = jnp.where(match, 1.0, 0.0).astype(BF16)
            for h in range(HALVES):
                pick[t, owner, c, h, j] = chosen[h * half : (h + 1) * half]

    def own_tables(t, carry):
        ranks([ids_own[t, k] for k in range(top)])
        for c in range(CHUNKS):
            choose(t, 0, c)
        return carry

    def pair_tables(t, carry):
        for c in range(CHUNKS):
            ranks([ids_pair[c, t, k] for k in range(top)])
            choose(t, 1, c)
        return carry

    def previous_tables(t, carry):
        ids = [ids_prev[t, k] for k in range(top)]
        ranks(ids)
        mix = jnp.zeros((peers, tokens), F32)
        for k in range(top):
            mix = jnp.where(ids[k] == expert_of, weights_prev[t, k], mix)
        mix_ref[...] = mix
        rows = []
        for k in range(peers):
            match = rank_ref[pl.ds(target[k], 1), :] == slot_of
            rows.append(jnp.where(match, mix_ref[pl.ds(target[k], 1), :], 0.0))
        for h in range(HALVES):
            half_rows = [row[h * half : (h + 1) * half] for row in rows]
            mixing[t, h] = jnp.concatenate(half_rows, axis=0).T.astype(BF16)
        return carry

    route.wait()
    own_tables(0, 0)
    for load in loads:
        load.wait()
    forwards = [
        pltpu.make_async_remote_copy(
            held, landing, route_send.at[i], route_recv.at[i],
            device_id={"section": following}, device_id_type=MESH,
        )
        for i, (held, landing) in enumerate([(ids_hbm, ids_prev), (weights_hbm, weights_prev)])
    ]
    pair_routes = [
        pltpu.make_async_remote_copy(
            ids_hbm, ids_pair.at[c], pair_send.at[c], pair_recv.at[c],
            device_id={"expert": partner[c]}, device_id_type=MESH,
        )
        for c in range(CHUNKS)
    ]

    def tick(t, carry):
        squares = jnp.zeros((tokens, 1), F32)
        for c in range(CHUNKS):
            h = hid[t, c].astype(F32)
            squares = squares + jnp.sum(h * h, axis=-1, keepdims=True)
        rescale = lax.rsqrt(squares / width + EPSILON)
        for c in range(CHUNKS):
            columns = slice(c * part, (c + 1) * part)
            normed[c] = (hid[t, c].astype(F32) * rescale * gain_ref[:, columns]).astype(BF16)

        @pl.when(t == 0)
        def _():
            pl.semaphore_wait(barrier, 3 * peers - 1)
            for pair_route in pair_routes:
                pair_route.start()

        shares = [
            pltpu.make_async_remote_copy(
                normed.at[c], dense.at[t, c], dense_send.at[c], dense_recv.at[t, c],
                device_id={"expert": partner[c]}, device_id_type=MESH,
            )
            for c in range(CHUNKS)
        ]
        for share in shares:
            share.start()
        carry_on = pltpu.make_async_remote_copy(
            hid.at[t], carried.at[t], carry_send, carry_recv.at[t],
            device_id={"section": following}, device_id_type=MESH,
        )

        def serve(owner, h, reverse=False):
            for c in range(CHUNKS):
                chosen = pick[t, owner, c, h].reshape(len(NEAR) * half, tokens)
                tokens_part = normed[c] if owner == 0 else dense[t, c]
                rows = jnp.dot(chosen, tokens_part, preferred_element_type=F32).astype(BF16)
                columns = slice(c * part, (c + 1) * part)
                rbuf[t, h, near_index[c][owner][0], :, columns] = rows[:half]
                for j in range(1, len(NEAR)):
                    sbuf[h, owner, c, j] = rows[j * half : (j + 1) * half]
            numbers = list(range(1, len(NEAR)))
            for j in reversed(numbers) if reverse else numbers:
                for c in range(CHUNKS):
                    pltpu.make_async_remote_copy(
                        sbuf.at[h, owner, c, j],
                        rbuf.at[t, h, near_index[c][owner][j], :, pl.ds(c * part, part)],
                        dispatch_send.at[h], dispatch_recv.at[t, h],
                        device_id={"expert": near_target[c][j]}, device_id_type=MESH,
                    ).start()

        serve(0, 0)
        carry_on.start()

        @pl.when(t == 0)
        def _():
            for forward in forwards:
                forward.start()
            for pair_route in pair_routes:
                pair_route.wait()
            pair_tables(0, 0)

        for share in shares:
            share.wait_recv()
        serve(1, 0)
        @pl.when(t == 0)
        def _():
            lax.fori_loop(1, ticks, own_tables, 0)
            lax.fori_loop(1, ticks, pair_tables, 0)

        serve(0, 1)
        serve(1, 1)

        @pl.when(t == 0)
        def _():
            inner_load.wait()
            outer_load.wait()

        arrivals = []
        returns = []
        remote = CHUNKS * 2 * (len(NEAR) - 1) * half * part // (half * width)
        for h in range(HALVES):
            landed = rbuf.at[t, h, pl.ds(0, remote)]
            arrival = pltpu.make_async_remote_copy(
                landed, landed, dispatch_send.at[h], dispatch_recv.at[t, h],
                device_id={"expert": partner[0]}, device_id_type=MESH,
            )
            arrival.wait_recv()
            arrivals.append(arrival)
            for n in range(ff // 256):
                gate_columns = slice(n * 256, (n + 1) * 256)
                up_columns = slice(ff + n * 256, ff + (n + 1) * 256)
                rows = rbuf[t, h].reshape(batch, width)
                gate = jnp.dot(rows, inner[:, gate_columns], preferred_element_type=F32)
                up = jnp.dot(rows, inner[:, up_columns], preferred_element_type=F32)
                act[:, gate_columns] = (gate / (1.0 + jnp.exp(-gate)) * up).astype(BF16)
            for r in range(RETURNS):
                for n in range(ret_part // part):
                    columns = slice(r * ret_part + n * part, r * ret_part + (n + 1) * part)
                    served = jnp.dot(act[...], outer[:, columns], preferred_element_type=F32).astype(BF16)
                    for k in range(peers):
                        obuf[h, r, k, :, n * part : (n + 1) * part] = served[k * half : (k + 1) * half]
                last = h == HALVES - 1 and r == RETURNS - 1
                for k in order:
                    pltpu.make_async_remote_copy(
                        obuf.at[h, r, k], ret.at[t, h, r, k], ret_send.at[h, r], ret_recv.at[t, h, r],
                        device_id={"section": following, "expert": source[k]}, device_id_type=MESH,
                    ).start()
                returns.append(
                    pltpu.make_async_remote_copy(
                        obuf.at[h, r], ret.at[t, h, r], ret_send.at[h, r], ret_recv.at[t, h, r],
                        device_id={"section": following, "expert": me}, device_id_type=MESH,
                    )
                )

        @pl.when(t == 0)
        def _():
            for forward in forwards:
                forward.wait()
            lax.fori_loop(0, ticks, previous_tables, 0)

        carry_on.wait_recv()
        for h in range(HALVES):
            for r in range(RETURNS):
                returns[h * RETURNS + r].wait_recv()
                for n in range(ret_part // part):
                    c = r * (ret_part // part) + n
                    rows = ret[t, h, r, :, :, n * part : (n + 1) * part].reshape(batch, part)
                    term = jnp.dot(mixing[t, h], rows, preferred_element_type=F32)
                    total = (carried[t, c].astype(F32) if h == 0 else acc[c]) + term
                    if h < HALVES - 1:
                        acc[c] = total
                    else:
                        hid[t + 1, c] = total.astype(BF16)
        for send in [*shares, *arrivals, *returns, carry_on]:
            send.wait_send()
        return carry

    lax.fori_loop(0, ticks, tick, 0)
    stores = [
        pltpu.make_async_copy(hid.at[ticks, c], out_ref.at[:, pl.ds(c * part, part)], out_sem.at[c])
        for c in range(CHUNKS)
    ]
    for store in stores:
        store.start()
    for store in stores:
        store.wait()


def on_device(state, norm_gain, expert_in, expert_out, route_ids, route_weights):
    hidden = state[0]
    tokens, width = hidden.shape
    ticks, top = route_ids.shape[0], route_ids.shape[3]
    ff = expert_out.shape[2]
    peers = SIDE * SIDE
    half = SLOTS // HALVES
    part = width // CHUNKS
    ret_part = width // RETURNS
    near = len(NEAR)
    vmem = pl.BlockSpec(memory_space=pltpu.VMEM)
    hbm = pl.BlockSpec(memory_space=pl.ANY)
    dma = pltpu.SemaphoreType.DMA
    result = pl.pallas_call(
        body,
        out_shape=jax.ShapeDtypeStruct((tokens, width), BF16),
        in_specs=[hbm, hbm, vmem, hbm, hbm, hbm],
        out_specs=hbm,
        scratch_shapes=[
            pltpu.VMEM((ticks, top, 1, tokens), jnp.int32),
            pltpu.VMEM((ticks, top, 1, tokens), jnp.int32),
            pltpu.VMEM((ticks, top, 1, tokens), F32),
            pltpu.VMEM((CHUNKS, ticks, top, 1, tokens), jnp.int32),
            pltpu.VMEM((ticks + 1, CHUNKS, tokens, part), BF16),
            pltpu.VMEM((ticks, CHUNKS, tokens, part), BF16),
            pltpu.VMEM((CHUNKS, tokens, part), BF16),
            pltpu.VMEM((ticks, CHUNKS, tokens, part), BF16),
            pltpu.VMEM((HALVES, 2, CHUNKS, near, half, part), BF16),
            pltpu.VMEM((ticks, HALVES, peers, half, width), BF16),
            pltpu.VMEM((HALVES, RETURNS, peers, half, ret_part), BF16),
            pltpu.VMEM((ticks, HALVES, RETURNS, peers, half, ret_part), BF16),
            pltpu.VMEM((CHUNKS, tokens, part), F32),
            pltpu.VMEM((width, 2 * ff), BF16),
            pltpu.VMEM((ff, width), BF16),
            pltpu.VMEM((peers * half, ff), BF16),
            pltpu.VMEM((peers, tokens), F32),
            pltpu.VMEM((peers, tokens), F32),
            pltpu.VMEM((ticks, 2, CHUNKS, HALVES, near, half, tokens), BF16),
            pltpu.VMEM((ticks, HALVES, tokens, peers * half), BF16),
            dma((CHUNKS,)),
            dma(()),
            dma((2,)),
            dma((CHUNKS,)),
            dma((2,)),
            dma((2,)),
            dma((CHUNKS,)),
            dma((CHUNKS,)),
            dma((CHUNKS,)),
            dma((ticks, CHUNKS)),
            dma((HALVES,)),
            dma((ticks, HALVES)),
            dma((HALVES, RETURNS)),
            dma((ticks, HALVES, RETURNS)),
            dma(()),
            dma((ticks,)),
        ],
        compiler_params=pltpu.CompilerParams(
            collective_id=0, has_side_effects=True, vmem_limit_bytes=56 * 1024 * 1024
        ),
    )(
        jnp.transpose(route_ids, (0, 3, 1, 2)),
        jnp.transpose(route_weights, (0, 3, 1, 2)),
        norm_gain,
        hidden,
        expert_in[0, 0],
        expert_out[0, 0],
    )
    return result[None]


def solution(mesh):
    in_specs = (
        P("section", "expert", None),
        P("section", None),
        P("section", "expert", None, None),
        P("section", "expert", None, None),
        P(None, "section", "expert", None),
        P(None, "section", "expert", None),
    )
    out_specs = P("section", "expert", None)
    return jax.shard_map(
        on_device, mesh=mesh, in_specs=in_specs, out_specs=out_specs, check_vma=False
    )
```

time: 160 us -> 156 us (0.975)
  the two profiles are of different devices: /device:TPU:66 before, /device:TPU:96 now
where the time goes in v4:
time: 156 us; the launch traced here: 155 us
  Pallas kernels  153 us (98%)
  local copies, waits for them, and re-layouts  1.88 us (1%)
    pallas_call x1, Pallas kernels, on_device(): pl.pallas_call(body, out_shape=jax.ShapeDtypeStruct((tokens, width), BF16...  153 us

profile of v4, /device:TPU:96, one launch (start us, length us, event | category | flops | bytes accessed | tf_op | source)
XLA Modules:
  0.0 155.3 jit_solution(7144383192534629192)
XLA Ops:
  0.0 153.5 %shard_map.64 = bf16[128,2048]{1,0:T(8,128)(2,1)} custom-call(s32[3,6,1,128]{3,2,1,0:T(1,128)} %bitcast.10, f32[3,6,1,128]{3,2,1,0:T(1,128)} %bitcast.11, f32[1,2048]{1,0:T(1,128)} %gain_ref.1, bf16[128,2048]{1,0:T(8,128)(2,1)} %bitcast.9, bf16[2048,1536]{1,0:T(8,128)(2,1)} %bitcast.6, bf16[768,2048]{1,0:T(8,128)(2,1)} %bitcast.7), custom_call_target="tpu_custom_call" | custom-call | tf_op jit(solution)/shard_map/pallas_call | solution.py:325
  153.5 1.9 %copy.8 = bf16[1,128,2048]{2,1,0:T(8,128)(2,1)} copy(bf16[1,128,2048]{2,1,0:T(8,128)(2,1)} %bitcast.8) | data formatting | bytes 1048576

commit v5 on v4

--- a/solution.py
+++ b/solution.py
@@ -159,6 +159,11 @@
             ids_hbm, ids_pair.at[c], pair_send.at[c], pair_recv.at[c],
             device_id={"expert": partner[c]}, device_id_type=MESH,
         )
+        for c in range(CHUNKS)
+    ]
+
+    stores = [
+        pltpu.make_async_copy(hid.at[ticks, c], out_ref.at[:, pl.ds(c * part, part)], out_sem.at[c])
         for c in range(CHUNKS)
     ]
 
@@ -294,17 +299,18 @@
                         acc[c] = total
                     else:
                         hid[t + 1, c] = total.astype(BF16)
+                        if c > 0:
+
+                            @pl.when(t == ticks - 1)
+                            def _(c=c):
+                                stores[c - 1].start()
+
         for send in [*shares, *arrivals, *returns, carry_on]:
             send.wait_send()
         return carry
 
     lax.fori_loop(0, ticks, tick, 0)
-    stores = [
-        pltpu.make_async_copy(hid.at[ticks, c], out_ref.at[:, pl.ds(c * part, part)], out_sem.at[c])
-        for c in range(CHUNKS)
-    ]
-    for store in stores:
-        store.start()
+    stores[-1].start()
     for store in stores:
         store.wait()
 

time: 156 us -> 155 us (level)
  no operation moved by 1% of the time
where the time goes in v5:
time: 155 us
  Pallas kernels  153 us (99%)
  local copies, waits for them, and re-layouts  1.88 us (1%)
    pallas_call x1, Pallas kernels, on_device(): pl.pallas_call(body, out_shape=jax.ShapeDtypeStruct((tokens, width), BF16...  153 us

profile of v5, /device:TPU:96, one launch (start us, length us, event | category | flops | bytes accessed | tf_op | source)
XLA Modules:
  0.0 155.2 jit_solution(13070301645366966722)
XLA Ops:
  0.0 153.4 %shard_map.64 = bf16[128,2048]{1,0:T(8,128)(2,1)} custom-call(s32[3,6,1,128]{3,2,1,0:T(1,128)} %bitcast.10, f32[3,6,1,128]{3,2,1,0:T(1,128)} %bitcast.11, f32[1,2048]{1,0:T(1,128)} %gain_ref.1, bf16[128,2048]{1,0:T(8,128)(2,1)} %bitcast.9, bf16[2048,1536]{1,0:T(8,128)(2,1)} %bitcast.6, bf16[768,2048]{1,0:T(8,128)(2,1)} %bitcast.7), custom_call_target="tpu_custom_call" | custom-call | tf_op jit(solution)/shard_map/pallas_call | solution.py:331
  153.4 1.9 %copy.8 = bf16[1,128,2048]{2,1,0:T(8,128)(2,1)} copy(bf16[1,128,2048]{2,1,0:T(8,128)(2,1)} %bitcast.8) | data formatting | bytes 1048576
